TPU v7x, 32 devices: a whole 2x2x4 slice. The times are simulated.
32 devices in a mesh: row: 8 (over z, core), col: 4 (over y, x).
Axes of the slice: x: 2, y: 2, z: 4, core: 2. Of those that a mesh axis runs over, the one named last changes fastest.
Arguments:
- signal: float32 [128, 128, 256], P(None, 'row', 'col'), may hold values from -6 to 6
- symbol_x: float32 [128], replicated, may hold values from 0.3 to 3
- symbol_y: float32 [128], replicated, may hold values from 0.3 to 3
- symbol_z: float32 [256], replicated, may hold values from 0.3 to 3
Outputs:
- modes: float32 [128, 128, 256], P('row', 'col')
All inputs are finite; a program needn't handle non-finite values.
Results may differ from a plain program's by a relative error of at most 0.0003.
Values sent between devices are 32-bit elements.
A program may use at most 64 MiB of HBM per device.

v0:
```python
import jax
import jax.numpy as jnp
from jax import lax
from jax.sharding import PartitionSpec as P


def mode_table(count):
    rank = jnp.arange(count)
    angle = 2.0 * jnp.pi / count * (rank[:, None] * rank[None, :] % count).astype(jnp.float32)
    return (jnp.cos(angle) + jnp.sin(angle)) * count ** (-0.5)


def transform_dim(values, dim):
    moved = jnp.tensordot(
        values, mode_table(values.shape[dim]), axes=([dim], [0]), precision=lax.Precision.HIGHEST
    )
    return jnp.moveaxis(moved, -1, dim)


def on_device(signal, symbol_x, symbol_y, symbol_z):

    def first_leg(part_values):
        part_values = transform_dim(part_values, 0)
        part_values = lax.all_to_all(part_values, "row", split_axis=0, concat_axis=1, tiled=True)
        part_values = transform_dim(part_values, 1)
        return part_values

    block_values = first_leg(signal)
    block_values = lax.all_to_all(block_values, "col", split_axis=1, concat_axis=2, tiled=True)
    block_values = transform_dim(block_values, 2)
    share_x = block_values.shape[0]
    part_x = lax.dynamic_slice_in_dim(symbol_x, lax.axis_index("row") * share_x, share_x)
    share_y = block_values.shape[1]
    part_y = lax.dynamic_slice_in_dim(symbol_y, lax.axis_index("col") * share_y, share_y)
    symbol = part_x[:, None, None] + part_y[None, :, None] + symbol_z[None, None, :]
    block_values = block_values * ((1.0 - 0.2 * symbol) / (1.0 + 0.2 * symbol))
    return block_values


def solution(mesh):
    placed = (P(None, "row", "col"), P(), P(), P())
    return jax.shard_map(
        on_device, mesh=mesh, in_specs=placed, out_specs=P("row", "col", None), check_vma=False
    )
```

profile of v0, /device:TPU:0, one launch (start us, length us, event | category | flops | bytes accessed | tf_op | source)
XLA Modules:
  0.0 49.0 jit_solution(2675580543085098439)
XLA Ops:
  0.0 1.0 %copy-done = f32[128,16,64]{0,2,1:T(8,128)S(1)} copy-done((f32[128,16,64]{0,2,1:T(8,128)S(1)}, f32[128,16,64]{0,2,1:T(8,128)}, u32[]{:S(2)}) %copy-start) | copy-done | bytes 524312
  1.0 0.8 %fusion.26 = f32[128,1024]{0,1:S(1)} fusion(f32[128,1024]{0,1:T(8,128)S(1)} %bitcast.22), kind=kOutput, calls=%fused_computation.32 | convolution fusion | flops 201588736 | bytes 1048576
  1.9 0.5 %copy.12 = f32[128,16,64]{2,1,0:T(8,128)S(1)} copy(f32[128,16,64]{0,2,1:T(8,128)S(1)} %bitcast.27) | data formatting | bytes 1048576 | tf_op jit(solution)/shard_map/dot_general | solution.py:14
  2.4 0.7 %reshape.37 = f32[8,1,16384]{2,1,0:T(1,128)S(1)} reshape(f32[128,16,64]{2,1,0:T(8,128)S(1)} %copy.12) | data formatting | bytes 1048576
  3.1 21.5 %all_to_all.36 = f32[8,1,16384]{2,1,0:T(1,128)S(1)} all-to-all(f32[8,1,16384]{2,1,0:T(1,128)S(1)} %reshape.37), channel_id=1, replica_groups=mesh['row'=8,'col'=4] {'row'}, dimensions={0} | all-to-all | bytes 1048576 | tf_op jit(solution)/shard_map/all_to_all | solution.py:24
  24.5 0.5 %broadcast.76 = f32[]{:T(128)} broadcast(f32[]{:T(128)} %constant.105), dimensions={} | broadcast | bytes 8 | tf_op jit(solution)/shard_map/all_to_all | solution.py:24
  25.0 1.8 %reduce = f32[8,16384]{1,0:T(8,128)S(1)} reduce(f32[8,1,16384]{2,1,0:T(1,128)S(1)} %all_to_all.36, f32[]{:T(128)} %broadcast.76), dimensions={1}, to_apply=%all_to_all.26.reduce_sub_computation | reduce | bytes 1048580 | tf_op jit(solution)/shard_map/all_to_all | solution.py:24
  26.8 0.4 reshape.38
  27.3 0.1 copy.13
  27.4 1.9 %convolution_bitcast_fusion = f32[16,128,64]{1,2,0:T(8,128)S(1)} fusion(f32[16,128,64]{2,1,0:T(8,128)S(1)} %bitcast.25), kind=kOutput, calls=%fused_computation | convolution fusion | flops 201588736 | bytes 1048576 | tf_op jit(solution)/shard_map/dot_general | solution.py:14
  29.3 0.5 %copy.15 = f32[16,128,64]{2,0,1:T(8,128)S(1)} copy(f32[16,128,64]{1,2,0:T(8,128)S(1)} %convolution_bitcast_fusion) | data formatting | bytes 1048576 | tf_op jit(solution)/shard_map/transpose | solution.py:17
  29.8 1.4 %reshape.39 = f32[4,1,32768]{2,1,0:T(1,128)} reshape(f32[128,16,64]{2,1,0:T(8,128)S(1)} %bitcast.23) | data formatting | bytes 1048576
  31.2 3.7 %all-to-all-start.1 = ((f32[4,1,32768]{2,1,0:T(1,128)}), f32[4,1,32768]{2,1,0:T(1,128)S(1)}, u32[]{:S(2)}, u32[]{:S(2)}) async-start(f32[4,1,32768]{2,1,0:T(1,128)} %reshape.39), calls=%async_computation.1 | async-start | bytes 1048576 | tf_op jit(solution)/shard_map/all_to_all | solution.py:29
  34.9 0.7 %copy-done.2 = f32[128]{0:T(128)S(1)} copy-done((f32[128]{0:T(128)S(1)}, f32[128]{0:T(128)}, u32[]{:S(2)}) %copy-start.2) | copy-done | bytes 536
  35.6 0.1 dynamic_slice.7
  35.7 0.7 %copy-done.3 = f32[128]{0:T(128)S(1)} copy-done((f32[128]{0:T(128)S(1)}, f32[128]{0:T(128)}, u32[]{:S(2)}) %copy-start.3) | copy-done | bytes 536
  36.3 0.1 dynamic_slice.6
  36.4 0.1 broadcast_add_fusion
  36.5 6.1 %all-to-all-done.1 = f32[4,1,32768]{2,1,0:T(1,128)S(1)} async-done(((f32[4,1,32768]{2,1,0:T(1,128)}), f32[4,1,32768]{2,1,0:T(1,128)S(1)}, u32[]{:S(2)}, u32[]{:S(2)}) %all-to-all-start.1) | async-done | bytes 524320 | tf_op jit(solution)/shard_map/all_to_all | solution.py:29
  42.6 2.1 %reduce.1 = f32[4,32768]{1,0:T(4,128)S(1)} reduce(f32[4,1,32768]{2,1,0:T(1,128)S(1)} %all-to-all-done.1, f32[]{:T(128)} %broadcast.76), dimensions={1}, to_apply=%all_to_all.30.reduce_sub_computation | reduce | bytes 1048580 | tf_op jit(solution)/shard_map/all_to_all | solution.py:29
  44.7 0.5 %reshape.40 = f32[128,16,64]{2,1,0:T(8,128)S(1)} reshape(f32[4,32768]{1,0:T(4,128)S(1)} %reduce.1) | data formatting | bytes 1048576
  45.2 0.7 %copy.17 = f32[16,32,4,64]{3,2,1,0:T(4,128)S(1)} copy(f32[16,32,4,64]{3,0,1,2:T(8,128)S(1)} %bitcast.26) | data formatting | bytes 1048576 | tf_op jit(solution)/shard_map/all_to_all | solution.py:29
  45.9 0.6 %all_to_all.33 = f32[16,32,256]{2,1,0:T(8,128)S(1)} reshape(f32[16,32,4,64]{3,2,1,0:T(4,128)S(1)} %copy.17) | data formatting | bytes 1048576 | tf_op jit(solution)/shard_map/all_to_all | solution.py:29
  46.6 2.4 %convolution_multiply_fusion = f32[16,32,256]{2,1,0:T(8,128)} fusion(f32[16,32,256]{2,1,0:T(8,128)S(1)} %all_to_all.33, f32[256]{0:T(256)S(1)} %copy-done.1, f32[16,32]{1,0:T(8,128)S(1)} %broadcast_add_fusion), kind=kOutput, calls=%fused_computation.1 | convolution fusion | flops 404488192 | bytes 1051648 | tf_op jit(solution)/shard_map/dot_general | solution.py:14
  (5 shorter events, 0.1 us)
Async XLA Ops:
  0.0 1.0 %copy-start = (f32[128,16,64]{0,2,1:T(8,128)S(1)}, f32[128,16,64]{0,2,1:T(8,128)}, u32[]{:S(2)}) copy-start(f32[128,16,64]{0,2,1:T(8,128)} %param.4) | copy-start | bytes 1572868
  31.2 11.4 %all-to-all-start.1 = ((f32[4,1,32768]{2,1,0:T(1,128)}), f32[4,1,32768]{2,1,0:T(1,128)S(1)}, u32[]{:S(2)}, u32[]{:S(2)}) async-start(f32[4,1,32768]{2,1,0:T(1,128)} %reshape.39), calls=%async_computation.1 | async-start | bytes 1048576 | tf_op jit(solution)/shard_map/all_to_all | solution.py:29
  34.9 0.7 %copy-start.2 = (f32[128]{0:T(128)S(1)}, f32[128]{0:T(128)}, u32[]{:S(2)}) copy-start(f32[128]{0:T(128)} %param.6) | copy-start | bytes 1540
  35.7 0.7 %copy-start.3 = (f32[128]{0:T(128)S(1)}, f32[128]{0:T(128)}, u32[]{:S(2)}) copy-start(f32[128]{0:T(128)} %param.5) | copy-start | bytes 1540
  45.9 0.7 %copy-start.1 = (f32[256]{0:T(256)S(1)}, f32[256]{0:T(256)}, u32[]{:S(2)}) copy-start(f32[256]{0:T(256)} %param.7) | copy-start | bytes 3076
where the time goes:
time: 49.3 us; the launch traced here: 49 us
  blocking collectives  21.5 us (44%)
  local copies, waits for them, and re-layouts  8.49 us (17%)
  waiting for transfers between devices  6.12 us (12%)
  matrix products  5.17 us (10%)
  other arithmetic  3.92 us (8%)
  starting transfers between devices  3.72 us (8%)
    all_to_all x1, blocking collectives, first_leg(): lax.all_to_all(part_values, 'row', split_axis=0, concat_axis=1, tiled=True)  21.5 us
    all_to_all x1, waiting for transfers between devices, on_device(): lax.all_to_all(block_values, 'col', split_axis=1, concat_axis=2, tiled=True)  6.12 us
    unnamed x12, local copies, waits for them, and re-layouts  5.44 us
    dot_general x2, matrix products, transform_dim(): jnp.tensordot(values, mode_table(values.shape[dim]), axes=([dim], [0]), p...  4.32 us
    all_to_all x1, starting transfers between devices, on_device(): lax.all_to_all(block_values, 'col', split_axis=1, concat_axis=2, tiled=True)  3.72 us
    all_to_all x1, other arithmetic, on_device(): lax.all_to_all(block_values, 'col', split_axis=1, concat_axis=2, tiled=True)  2.05 us
    all_to_all x1, other arithmetic, first_leg(): lax.all_to_all(part_values, 'row', split_axis=0, concat_axis=1, tiled=True)  1.8 us
    all_to_all x2, local copies, waits for them, and re-layouts, on_device(): lax.all_to_all(block_values, 'col', split_axis=1, concat_axis=2, tiled=True)  1.29 us
  transfers between devices with their start and end apart: 1, of which 1 were waited for; matrix products, arithmetic and copies ran while one was open for 0% of the time, Pallas kernels for 0%

commit v1 on v0

--- a/solution.py
+++ b/solution.py
@@ -21,7 +21,10 @@
 
     def first_leg(part_values):
         part_values = transform_dim(part_values, 0)
-        part_values = lax.all_to_all(part_values, "row", split_axis=0, concat_axis=1, tiled=True)
+        masks_handle = lambda x_part, across: jnp.concatenate(
+            lax.all_to_all(jnp.stack(jnp.split(x_part, lax.axis_size(across), 0)), across, 0, 0), 1
+        )
+        part_values = masks_handle(part_values, "row")
         part_values = transform_dim(part_values, 1)
         return part_values
 

time: 49.3 us -> 57.7 us (1.17)
  local copies, waits for them, and re-layouts: 8.49 us -> 16.4 us
    another operation x0 -> x10, local copies, waits for them, and re-layouts: none -> 7.49 us  [first_leg(): jnp.stack(jnp.split(x_part, lax.axis_size(across), 0))]
    unnamed x12 -> x21, local copies, waits for them, and re-layouts: 5.44 us -> 6.33 us
where the time goes in v1:
time: 57.7 us; the launch traced here: 57.3 us
  blocking collectives  21.5 us (37%)
  local copies, waits for them, and re-layouts  16.4 us (28%)
  waiting for transfers between devices  6.19 us (11%)
  matrix products  5.17 us (9%)
  other arithmetic  4.07 us (7%)
  starting transfers between devices  3.72 us (6%)
    all_to_all x1, blocking collectives, first_leg(): lax.all_to_all(jnp.stack(jnp.split(x_part, lax.axis_size(across), 0)), ac...  21.5 us
    another operation x10, local copies, waits for them, and re-layouts, first_leg(): jnp.stack(jnp.split(x_part, lax.axis_size(across), 0))  7.49 us
    unnamed x21, local copies, waits for them, and re-layouts  6.33 us
    all_to_all x1, waiting for transfers between devices, on_device(): lax.all_to_all(block_values, 'col', split_axis=1, concat_axis=2, tiled=True)  6.19 us
    dot_general x2, matrix products, transform_dim(): jnp.tensordot(values, mode_table(values.shape[dim]), axes=([dim], [0]), p...  4.33 us
    all_to_all x1, starting transfers between devices, on_device(): lax.all_to_all(block_values, 'col', split_axis=1, concat_axis=2, tiled=True)  3.72 us
    all_to_all x1, other arithmetic, on_device(): lax.all_to_all(block_values, 'col', split_axis=1, concat_axis=2, tiled=True)  2.13 us
    all_to_all x1, other arithmetic, first_leg(): lax.all_to_all(jnp.stack(jnp.split(x_part, lax.axis_size(across), 0)), ac...  1.87 us
  transfers between devices with their start and end apart: 1, of which 1 were waited for; matrix products, arithmetic and copies ran while one was open for 0% of the time, Pallas kernels for 0%

profile of v1, /device:TPU:0, one launch (start us, length us, event | category | flops | bytes accessed | tf_op | source)
XLA Modules:
  0.0 57.3 jit_solution(10865362876156333967)
XLA Ops:
  0.0 1.0 %copy-done = f32[128,16,64]{0,2,1:T(8,128)S(1)} copy-done((f32[128,16,64]{0,2,1:T(8,128)S(1)}, f32[128,16,64]{0,2,1:T(8,128)}, u32[]{:S(2)}) %copy-start) | copy-done | bytes 524312
  1.0 0.8 %fusion.26 = f32[128,1024]{0,1:S(1)} fusion(f32[128,1024]{0,1:T(8,128)S(1)} %bitcast.36), kind=kOutput, calls=%fused_computation.40 | convolution fusion | flops 201588736 | bytes 1048576
  1.9 2.1 %slice_bitcast_fusion = (f32[1,16,16,64]{1,3,2,0:T(8,128)}, f32[1,16,16,64]{1,3,2,0:T(8,128)}, f32[1,16,16,64]{1,3,2,0:T(8,128)}, f32[1,16,16,64]{1,3,2,0:T(8,12...) fusion(f32[128,16,64]{0,2,1:T(8,128)S(1)} %bitcast.37), kind=kLoop, calls=%fused_computation.2 | loop fusion | bytes 1048576 | tf_op jit(solution)/shard_map/stack | solution.py:25
  4.0 1.2 %copy.29 = f32[1,16,16,64]{3,2,1,0:T(8,128)S(1)} copy(f32[1,16,16,64]{1,3,2,0:T(8,128)} %get-tuple-element.5) | data formatting | bytes 131072 | tf_op jit(solution)/shard_map/stack | solution.py:25
  5.3 1.2 %copy.28 = f32[1,16,16,64]{3,2,1,0:T(8,128)S(1)} copy(f32[1,16,16,64]{1,3,2,0:T(8,128)} %get-tuple-element.6) | data formatting | bytes 131072 | tf_op jit(solution)/shard_map/stack | solution.py:25
  6.5 1.2 %copy.27 = f32[1,16,16,64]{3,2,1,0:T(8,128)S(1)} copy(f32[1,16,16,64]{1,3,2,0:T(8,128)} %get-tuple-element.7) | data formatting | bytes 131072 | tf_op jit(solution)/shard_map/stack | solution.py:25
  7.8 0.8 %copy.26 = f32[1,16,16,64]{3,2,1,0:T(8,128)} copy(f32[1,16,16,64]{1,3,2,0:T(8,128)S(1)} %get-tuple-element.8) | data formatting | bytes 131072 | tf_op jit(solution)/shard_map/stack | solution.py:25
  9.5 0.9 %copy-done.1 = f32[1,16,16,64]{3,2,1,0:T(8,128)S(1)} copy-done((f32[1,16,16,64]{3,2,1,0:T(8,128)S(1)}, f32[1,16,16,64]{3,2,1,0:T(8,128)}, u32[]{:S(2)}) %copy-start.1) | copy-done | bytes 65560
  10.4 0.7 %reshape.45 = f32[8,1,16384]{2,1,0:T(1,128)S(1)} reshape(f32[8,16,16,64]{3,2,1,0:T(8,128)S(1)} %constant_dynamic-update-slice_fusion) | data formatting | bytes 1048576
  11.1 21.5 %all_to_all.23 = f32[8,1,16384]{2,1,0:T(1,128)S(1)} all-to-all(f32[8,1,16384]{2,1,0:T(1,128)S(1)} %reshape.45), channel_id=1, replica_groups=mesh['row'=8,'col'=4] {'row'}, dimensions={0} | all-to-all | bytes 1048576 | tf_op jit(solution)/shard_map/all_to_all | solution.py:25
  32.6 0.6 %broadcast.76 = f32[]{:T(128)} broadcast(f32[]{:T(128)} %constant.128), dimensions={} | broadcast | bytes 8 | tf_op jit(solution)/shard_map/all_to_all | solution.py:25
  33.2 1.9 %reduce = f32[8,16384]{1,0:T(8,128)S(1)} reduce(f32[8,1,16384]{2,1,0:T(1,128)S(1)} %all_to_all.23, f32[]{:T(128)} %broadcast.76), dimensions={1}, to_apply=%all_to_all.16.reduce_sub_computation | reduce | bytes 1048580 | tf_op jit(solution)/shard_map/all_to_all | solution.py:25
  35.6 1.9 %convolution_bitcast_fusion = f32[16,128,64]{1,2,0:T(8,128)S(1)} fusion(f32[16,128,64]{2,1,0:T(8,128)S(1)} %bitcast.40), kind=kOutput, calls=%fused_computation | convolution fusion | flops 201588736 | bytes 1048576 | tf_op jit(solution)/shard_map/dot_general | solution.py:14
  37.5 0.5 copy.32
  38.0 1.4 %reshape.47 = f32[4,1,32768]{2,1,0:T(1,128)} reshape(f32[128,16,64]{2,1,0:T(8,128)S(1)} %bitcast.38) | data formatting | bytes 1048576
  39.4 3.7 %all-to-all-start.1 = ((f32[4,1,32768]{2,1,0:T(1,128)}), f32[4,1,32768]{2,1,0:T(1,128)S(1)}, u32[]{:S(2)}, u32[]{:S(2)}) async-start(f32[4,1,32768]{2,1,0:T(1,128)} %reshape.47), calls=%async_computation.1 | async-start | bytes 1048576 | tf_op jit(solution)/shard_map/all_to_all | solution.py:32
  43.1 0.7 %copy-done.3 = f32[128]{0:T(128)S(1)} copy-done((f32[128]{0:T(128)S(1)}, f32[128]{0:T(128)}, u32[]{:S(2)}) %copy-start.3) | copy-done | bytes 536
  43.9 0.6 %copy-done.4 = f32[128]{0:T(128)S(1)} copy-done((f32[128]{0:T(128)S(1)}, f32[128]{0:T(128)}, u32[]{:S(2)}) %copy-start.4) | copy-done | bytes 536
  44.6 6.2 %all-to-all-done.1 = f32[4,1,32768]{2,1,0:T(1,128)S(1)} async-done(((f32[4,1,32768]{2,1,0:T(1,128)}), f32[4,1,32768]{2,1,0:T(1,128)S(1)}, u32[]{:S(2)}, u32[]{:S(2)}) %all-to-all-start.1) | async-done | bytes 524320 | tf_op jit(solution)/shard_map/all_to_all | solution.py:32
  50.8 2.1 %reduce.1 = f32[4,32768]{1,0:T(4,128)S(1)} reduce(f32[4,1,32768]{2,1,0:T(1,128)S(1)} %all-to-all-done.1, f32[]{:T(128)} %broadcast.76), dimensions={1}, to_apply=%all_to_all.17.reduce_sub_computation | reduce | bytes 1048580 | tf_op jit(solution)/shard_map/all_to_all | solution.py:32
  52.9 0.5 reshape.48
  53.4 0.7 %copy.34 = f32[16,32,4,64]{3,2,1,0:T(4,128)S(1)} copy(f32[16,32,4,64]{3,0,1,2:T(8,128)S(1)} %bitcast.41) | data formatting | bytes 1048576 | tf_op jit(solution)/shard_map/all_to_all | solution.py:32
  54.1 0.6 %all_to_all.20 = f32[16,32,256]{2,1,0:T(8,128)S(1)} reshape(f32[16,32,4,64]{3,2,1,0:T(4,128)S(1)} %copy.34) | data formatting | bytes 1048576 | tf_op jit(solution)/shard_map/all_to_all | solution.py:32
  54.8 2.4 %convolution_multiply_fusion = f32[16,32,256]{2,1,0:T(8,128)} fusion(f32[16,32,256]{2,1,0:T(8,128)S(1)} %all_to_all.20, f32[256]{0:T(256)S(1)} %copy-done.2, f32[16,32]{1,0:T(8,128)S(1)} %broadcast_add_fusion), kind=kOutput, calls=%fused_computation.1 | convolution fusion | flops 404488192 | bytes 1051648 | tf_op jit(solution)/shard_map/dot_general | solution.py:14
  (23 shorter events, 1.7 us)
Async XLA Ops:
  0.0 1.0 %copy-start = (f32[128,16,64]{0,2,1:T(8,128)S(1)}, f32[128,16,64]{0,2,1:T(8,128)}, u32[]{:S(2)}) copy-start(f32[128,16,64]{0,2,1:T(8,128)} %param.4) | copy-start | bytes 1572868
  9.5 0.9 %copy-start.1 = (f32[1,16,16,64]{3,2,1,0:T(8,128)S(1)}, f32[1,16,16,64]{3,2,1,0:T(8,128)}, u32[]{:S(2)}) copy-start(f32[1,16,16,64]{3,2,1,0:T(8,128)} %copy.26) | copy-start | bytes 196612
  39.4 11.4 %all-to-all-start.1 = ((f32[4,1,32768]{2,1,0:T(1,128)}), f32[4,1,32768]{2,1,0:T(1,128)S(1)}, u32[]{:S(2)}, u32[]{:S(2)}) async-start(f32[4,1,32768]{2,1,0:T(1,128)} %reshape.47), calls=%async_computation.1 | async-start | bytes 1048576 | tf_op jit(solution)/shard_map/all_to_all | solution.py:32
  43.1 0.7 %copy-start.3 = (f32[128]{0:T(128)S(1)}, f32[128]{0:T(128)}, u32[]{:S(2)}) copy-start(f32[128]{0:T(128)} %param.6) | copy-start | bytes 1540
  43.8 0.7 %copy-start.4 = (f32[128]{0:T(128)S(1)}, f32[128]{0:T(128)}, u32[]{:S(2)}) copy-start(f32[128]{0:T(128)} %param.5) | copy-start | bytes 1540
  54.1 0.7 %copy-start.2 = (f32[256]{0:T(256)S(1)}, f32[256]{0:T(256)}, u32[]{:S(2)}) copy-start(f32[256]{0:T(256)} %param.7) | copy-start | bytes 3076
